TPU v7x, 256 devices: a whole 4x4x8 slice. The times are simulated.
256 devices in a mesh: gz: 64 (over z, x, core), col: 4 (over y).
Axes of the slice: x: 4, y: 4, z: 8, core: 2. Of those that a mesh axis runs over, the one named last changes fastest.
Arguments:
- source: float32 [4096, 2048], P('gz', 'col'), may hold values from -6 to 6
- z_vectors: float32 [4096, 4096], P('gz', 'col'), may hold values from -0.25 to 0.25
- x_vectors: float32 [4, 4], replicated, may hold values from -3 to 3
- y_vectors: float32 [512, 512], replicated, may hold values from -0.25 to 0.25
- z_values: float32 [4096], replicated, may hold values from 0.1 to 3
- x_values: float32 [4], replicated, may hold values from 0.1 to 3
- y_values: float32 [512], replicated, may hold values from 0.1 to 3
Outputs:
- solution: float32 [4096, 2048], P('gz', 'col')
All inputs are finite; a program needn't handle non-finite values.
Results may differ from a plain program's by a relative error of at most 0.000092.
Values sent between devices are 32-bit elements; how exact they have to be, the bound alone decides.
A program may use at most 64 MiB of HBM per device.

v0:
```python
import jax
import jax.numpy as jnp
from jax import lax
from jax.sharding import Mesh
from jax.sharding import PartitionSpec as P

GZ = ("gz_0", "gz_1", "gz_2")
exact_mode = lax.Precision.HIGHEST


def in_order(pieces, dim):
    shape = list(pieces.shape[1:])
    shape[dim] *= pieces.shape[0]
    return jnp.moveaxis(pieces, 0, dim).reshape(shape)


def sent_to_all(value, axis):
    devices = lax.axis_size(axis)
    return lax.all_to_all(
        jnp.broadcast_to(value[None], (devices, *value.shape)), axis, 0, 0, tiled=True
    )


def gather_directly(value, axis, dim):
    return in_order(sent_to_all(value, axis), dim)


def own_rows(subtotal, axes):
    for axis in axes:
        subtotal = lax.psum_scatter(subtotal, axis, scatter_dimension=0, tiled=True)
    return subtotal


def cut_along(value, dim, devices):
    shape = value.shape
    pieces = value.reshape(*shape[:dim], devices, shape[dim] // devices, *shape[dim + 1 :])
    return jnp.moveaxis(pieces, dim, 0)


def sum_at_owner(value, axis, dim):
    devices = lax.axis_size(axis)
    pieces = lax.all_to_all(cut_along(value, dim, devices), axis, 0, 0, tiled=True)
    return jnp.sum(pieces, axis=0)


def lead_product(left_side, right_side):
    return lax.dot_general(
        left_side,
        right_side,
        (((0,), (0,)), ((), ())),
        precision=exact_mode,
        preferred_element_type=jnp.float32,
    )


def shards(source, z_vectors, x_vectors, y_vectors, z_values, x_values, y_values):
    z_rows = source.shape[0]
    width_y = y_vectors.shape[0]
    width_x = x_vectors.shape[0]
    x_lines = source.shape[1] // width_y
    column = lax.axis_index("col")
    row_block = lax.axis_index(GZ)
    along_y = jnp.dot(source, y_vectors, precision=exact_mode, preferred_element_type=jnp.float32)
    planes = gather_directly(along_y, "col", 1)
    modal_full = jnp.einsum(
        "zxj,xi->zij", planes.reshape(z_rows, width_x, width_y), x_vectors, precision=exact_mode
    )
    modal_full = modal_full.reshape(z_rows, width_x * width_y)
    part_rows = z_rows // lax.axis_size("col")
    coeffs = own_rows(lead_product(z_vectors, modal_full), GZ)
    mode_start = column * z_vectors.shape[1] + row_block * part_rows
    z_part = lax.dynamic_slice_in_dim(z_values, mode_start, part_rows, 0)
    divisor = z_part[:, None, None] + x_values[None, :, None] + y_values[None, None, :]
    scaled = (coeffs.reshape(part_rows, width_x, width_y) / divisor).reshape(
        part_rows, width_x * width_y
    )
    back_z = jnp.dot(
        z_vectors,
        lax.all_gather(scaled, GZ, axis=0, tiled=True),
        precision=exact_mode,
        preferred_element_type=jnp.float32,
    )
    spread_x = jnp.einsum(
        "zij,xi->zxj", back_z.reshape(z_rows, width_x, width_y), x_vectors, precision=exact_mode
    )
    summed = sum_at_owner(spread_x.reshape(z_rows, width_x * width_y), "col", 1)
    back_x = summed.reshape(z_rows, x_lines, width_y)
    solution = lax.dot_general(
        back_x.reshape(z_rows * x_lines, width_y),
        y_vectors,
        (((1,), (1,)), ((), ())),
        precision=exact_mode,
        preferred_element_type=jnp.float32,
    )
    return solution


def solution(mesh):
    torus = Mesh(mesh.devices.reshape(8, 4, 2, mesh.shape["col"]), ("gz_0", "gz_1", "gz_2", "col"))
    return jax.shard_map(
        shards,
        mesh=torus,
        in_specs=(P(GZ, "col"), P(GZ, "col"), P(), P(), P(), P(), P()),
        out_specs=P(GZ, "col"),
        check_vma=False,
    )
```

profile of v0, /device:TPU:1, one launch (start us, length us, event | category | flops | bytes accessed | tf_op | source)
XLA Modules:
  0.0 293.1 jit_solution(16918401710747406262)
XLA Ops:
  6.5 0.0 copy-start
  6.5 0.0 reduce-scatter.8.cloned.1.call-start
  6.5 1.2 copy-done
  7.8 1.7 fusion.7
  9.4 0.1 broadcast_in_dim.2
  9.5 13.4 %all_to_all.10 = f32[4,64,512]{2,1,0:T(8,128)S(1)} all-to-all(f32[4,64,512]{2,1,0:T(8,128)S(1)} %broadcast_in_dim.2), channel_id=1, replica_groups=mesh['gz_0'=8,'gz_1'=4,'gz_2'=2,'col'=4] {'col'}, dimensions={0} | all-to-all | bytes 1048576 | tf_op jit(solution)/shard_map/all_to_all | solution.py:19
  22.9 2.0 fusion.1
  24.9 0.2 copy.19
  25.1 10.0 %convolution_bitcast_fusion = f32[1024,2048]{0,1:T(8,128)} fusion(f32[64,2048]{1,0:T(8,128)S(1)} %bitcast.37, f32[64,1024]{1,0:T(8,128)} %param.8), kind=kOutput, calls=%fused_computation | convolution fusion | flops 1610612736 | bytes 9175040 | tf_op jit(solution)/shard_map/dot_general | solution.py:47
  35.1 0.0 copy-start.3
  35.1 0.0 copy-start.4
  35.1 0.0 copy-start.1
  35.1 0.0 reduce-scatter.8.cloned.1.call-update
  35.1 0.0 reduce-scatter.10.cloned.1.call-start
  35.2 97.1 %reduce-scatter.8.cloned.1.call-done = f32[128,2048]{0,1:T(8,128)} async-done(((f32[1024,2048]{0,1:T(8,128)}), f32[128,2048]{0,1:T(8,128)}) %reduce-scatter.8.cloned.1.call-update) | async-done | bytes 1048592 | tf_op jit(solution)/shard_map/reduce_scatter | solution.py:30
  132.2 2.5 copy.15
  134.8 0.0 copy-start.2
  134.8 0.0 reduce-scatter.10.cloned.1.call-update
  134.8 0.0 reduce-scatter.12.cloned.1.call-start
  134.8 23.6 %reduce-scatter.10.cloned.1.call-done = f32[32,2048]{1,0:T(8,128)} async-done(((f32[128,2048]{1,0:T(8,128)}), f32[32,2048]{1,0:T(8,128)}) %reduce-scatter.10.cloned.1.call-update) | async-done | bytes 262160
  158.5 0.0 reduce-scatter.12.cloned.1.call-update
  158.5 0.0 all-gather.2.cloned.1.call-start
  158.5 0.0 copy-done.3
  158.6 0.8 dynamic_slice.3
  159.3 0.0 copy-done.4
  159.3 0.1 broadcast_add_fusion
  159.4 16.6 %reduce-scatter.12.cloned.1.call-done = f32[16,2048]{1,0:T(8,128)} async-done(((f32[32,2048]{1,0:T(8,128)}), f32[16,2048]{1,0:T(8,128)}) %reduce-scatter.12.cloned.1.call-update) | async-done | bytes 131088
  176.0 1.2 copy.18
  177.2 0.3 fusion
  177.6 1.0 copy.11
  178.5 0.0 all-gather.2.cloned.1.call-update
  178.6 84.0 %all-gather.2.cloned.1.call-done = f32[1024,2048]{1,0:T(8,128)} async-done(((f32[16,2048]{1,0:T(8,128)}), f32[1024,2048]{1,0:T(8,128)}) %all-gather.2.cloned.1.call-update) | async-done | bytes 8388624 | tf_op jit(solution)/shard_map/all_gather | solution.py:79
  262.6 0.0 copy-done.1
  262.6 7.8 %convolution_bitcast_fusion.1 = f32[64,2048]{1,0:T(8,128)S(1)} fusion(f32[1024,2048]{1,0:T(8,128)} %all-gather.2.cloned.1.call-done, f32[64,1024]{1,0:T(8,128)S(1)} %copy-done.1), kind=kOutput, calls=%fused_computation.1 | convolution fusion | flops 1610612736 | bytes 9175040 | tf_op jit(solution)/shard_map/dot_general | solution.py:77
  270.4 0.4 reshape.45
  270.7 0.0 copy-done.2
  270.7 1.0 fusion.4
  271.8 0.2 copy.26
  271.9 12.8 %all_to_all.11 = f32[4,64,512]{2,1,0:T(8,128)S(1)} all-to-all(f32[4,64,512]{2,1,0:T(8,128)S(1)} %bitcast.39), channel_id=1, replica_groups=mesh['gz_0'=8,'gz_1'=4,'gz_2'=2,'col'=4] {'col'}, dimensions={0} | all-to-all | bytes 1048576 | tf_op jit(solution)/shard_map/all_to_all | solution.py:42
  284.8 1.8 fusion.8
  (3 shorter events, 0.0 us)
Async XLA Ops:
  6.5 1.2 copy-start
  6.5 125.7 %reduce-scatter.8.cloned.1.call-start = ((), (), s32[]{:S(2)}) async-start(), calls=%async_computation.5 | async-start | bytes 9437184 | tf_op jit(solution)/shard_map/reduce_scatter | solution.py:30
  35.1 123.4 %copy-start.3 = (f32[512]{0:T(512)S(1)}, f32[512]{0:T(512)}, u32[]{:S(2)}) copy-start(f32[512]{0:T(512)} %param.13) | copy-start | bytes 6148
  35.1 124.2 %copy-start.4 = (f32[4]{0:T(128)S(1)}, f32[4]{0:T(128)}, u32[]{:S(2)}) copy-start(f32[4]{0:T(128)} %param.12) | copy-start | bytes 52
  35.1 227.5 %copy-start.1 = (f32[64,1024]{1,0:T(8,128)S(1)}, f32[64,1024]{1,0:T(8,128)}, u32[]{:S(2)}) copy-start(f32[64,1024]{1,0:T(8,128)} %param.8) | copy-start | bytes 786436
  35.1 123.3 %reduce-scatter.10.cloned.1.call-start = ((), (), s32[]{:S(2)}) async-start(), calls=%async_computation.7 | async-start | bytes 1310720
  134.8 136.0 %copy-start.2 = (f32[4,4]{1,0:T(4,128)S(1)}, f32[4,4]{1,0:T(4,128)}, u32[]{:S(2)}) copy-start(f32[4,4]{1,0:T(4,128)} %param.9) | copy-start | bytes 196
  134.8 41.2 %reduce-scatter.12.cloned.1.call-start = ((), (), s32[]{:S(2)}) async-start(), calls=%async_computation.8 | async-start | bytes 393216
  158.5 104.1 %all-gather.2.cloned.1.call-start = ((), (), s32[]{:S(2)}) async-start(), calls=%async_computation.6 | async-start | bytes 8519680 | tf_op jit(solution)/shard_map/all_gather | solution.py:79
Sparse Core Ops, SparseCore 0:
  35.3 96.9 reduce-scatter.7
  134.9 23.4 reduce-scatter.9
  160.9 14.9 reduce-scatter.11
  178.7 83.8 all-gather.1
where the time goes:
time: 293 us
  waiting for transfers between devices  221 us (75%)
  blocking collectives  26.3 us (9%)
  matrix products  24.3 us (8%)
  between operations  13.3 us (5%)
  local copies, waits for them, and re-layouts  7.47 us (3%)
    reduce_scatter x1, waiting for transfers between devices, own_rows(): subtotal = lax.psum_scatter(subtotal, axis, scatter_dimension=0, tiled=True)  97.1 us
    all_gather x1, waiting for transfers between devices, shards(): lax.all_gather(scaled, GZ, axis=0, tiled=True)  84 us
    unnamed x6, waiting for transfers between devices  40.2 us
    all_to_all x1, blocking collectives, sent_to_all(): lax.all_to_all(jnp.broadcast_to(value[None], (devices, *value.shape)), ax...  13.4 us
    all_to_all x1, blocking collectives, sum_at_owner(): lax.all_to_all(cut_along(value, dim, devices), axis, 0, 0, tiled=True)  12.8 us
    dot_general x1, matrix products, lead_product(): lax.dot_general(left_side, right_side, (((0,), (0,)), ((), ())), precisio...  10 us
    dot_general x1, matrix products, shards(): jnp.dot(z_vectors, lax.all_gather(scaled, GZ, axis=0, tiled=True), precis...  7.81 us
  transfers between devices with their start and end apart: 4, of which 4 were waited for; matrix products, arithmetic and copies ran while one was open for 0% of the time, Pallas kernels for 0%

commit v1 on v0

--- a/solution.py
+++ b/solution.py
@@ -6,6 +6,11 @@
 
 GZ = ("gz_0", "gz_1", "gz_2")
 exact_mode = lax.Precision.HIGHEST
+
+
+def all_by_exchange(shard, name, dim):
+    outgoing = jnp.stack([shard] * lax.axis_size(name))
+    return jnp.concatenate(lax.all_to_all(outgoing, name, 0, 0), axis=dim)
 
 
 def in_order(pieces, dim):
@@ -76,7 +81,7 @@
     )
     back_z = jnp.dot(
         z_vectors,
-        lax.all_gather(scaled, GZ, axis=0, tiled=True),
+        all_by_exchange(scaled, GZ, 0),
         precision=exact_mode,
         preferred_element_type=jnp.float32,
     )

time: 293 us -> 402 us (1.37)
  blocking collectives: 26.3 us -> 219 us
  waiting for transfers between devices: 221 us -> 137 us
    all_to_all x0 -> x1, blocking collectives: none -> 194 us  [all_by_exchange(): return jnp.concatenate(lax.all_to_all(outgoing, name, 0, 0), axis=dim)]
    all_gather x1 -> x0, waiting for transfers between devices: 84 us -> none  [shards(): lax.all_gather(scaled, GZ, axis=0, tiled=True)]
    unnamed x6 -> x5, waiting for transfers between devices: 40.2 us -> 40.3 us
  transfers between devices with their start and end apart: 4 -> 3, of which waited for: 4 -> 3; matrix products, arithmetic and copies ran while one was open for 0% -> 0% of each run, Pallas kernels for 0% -> 0%
where the time goes in v1:
time: 402 us; the launch traced here: 399 us
  blocking collectives  219 us (54%)
  waiting for transfers between devices  137 us (34%)
  matrix products  21.9 us (5%)
  between operations  13.2 us (3%)
  local copies, waits for them, and re-layouts  7.85 us (2%)
    all_to_all x1, blocking collectives, all_by_exchange(): return jnp.concatenate(lax.all_to_all(outgoing, name, 0, 0), axis=dim)  194 us
    reduce_scatter x1, waiting for transfers between devices, own_rows(): subtotal = lax.psum_scatter(subtotal, axis, scatter_dimension=0, tiled=True)  97.1 us
    unnamed x5, waiting for transfers between devices  40.3 us
    all_to_all x1, blocking collectives, sent_to_all(): lax.all_to_all(jnp.broadcast_to(value[None], (devices, *value.shape)), ax...  13.4 us
    all_to_all x1, blocking collectives, sum_at_owner(): lax.all_to_all(cut_along(value, dim, devices), axis, 0, 0, tiled=True)  10.7 us
    dot_general x1, matrix products, lead_product(): lax.dot_general(left_side, right_side, (((0,), (0,)), ((), ())), precisio...  9.94 us
  transfers between devices with their start and end apart: 3, of which 3 were waited for; matrix products, arithmetic and copies ran while one was open for 0% of the time, Pallas kernels for 0%

profile of v1, /device:TPU:1, one launch (start us, length us, event | category | flops | bytes accessed | tf_op | source)
XLA Modules:
  0.0 399.4 jit_solution(13178243082120037823)
XLA Ops:
  6.5 0.0 copy-start
  6.5 0.0 reduce-scatter.8.cloned.1.call-start
  6.5 1.2 copy-done
  7.8 1.7 fusion.7
  9.4 0.1 broadcast_in_dim.2
  9.5 13.4 %all_to_all.15 = f32[4,64,512]{2,1,0:T(8,128)S(1)} all-to-all(f32[4,64,512]{2,1,0:T(8,128)S(1)} %broadcast_in_dim.2), channel_id=1, replica_groups=mesh['gz_0'=8,'gz_1'=4,'gz_2'=2,'col'=4] {'col'}, dimensions={0} | all-to-all | bytes 1048576 | tf_op jit(solution)/shard_map/all_to_all | solution.py:24
  22.9 2.0 fusion.1
  24.9 0.2 copy.20
  25.1 9.9 %convolution_bitcast_fusion = f32[1024,2048]{0,1:T(8,128)} fusion(f32[64,2048]{1,0:T(8,128)S(1)} %bitcast.39, f32[64,1024]{1,0:T(8,128)} %param.8), kind=kOutput, calls=%fused_computation | convolution fusion | flops 1610612736 | bytes 9175040 | tf_op jit(solution)/shard_map/dot_general | solution.py:52
  35.0 0.0 copy-start.3
  35.0 0.0 copy-start.4
  35.0 0.0 reduce-scatter.8.cloned.1.call-update
  35.0 0.0 reduce-scatter.10.cloned.1.call-start
  35.1 97.1 %reduce-scatter.8.cloned.1.call-done = f32[128,2048]{0,1:T(8,128)} async-done(((f32[1024,2048]{0,1:T(8,128)}), f32[128,2048]{0,1:T(8,128)}) %reduce-scatter.8.cloned.1.call-update) | async-done | bytes 1048592 | tf_op jit(solution)/shard_map/reduce_scatter | solution.py:35
  132.1 2.5 copy.16
  134.7 0.0 reduce-scatter.10.cloned.1.call-update
  134.7 0.0 reduce-scatter.12.cloned.1.call-start
  134.8 23.6 %reduce-scatter.10.cloned.1.call-done = f32[32,2048]{1,0:T(8,128)} async-done(((f32[128,2048]{1,0:T(8,128)}), f32[32,2048]{1,0:T(8,128)}) %reduce-scatter.10.cloned.1.call-update) | async-done | bytes 262160
  158.3 0.0 reduce-scatter.12.cloned.1.call-update
  158.3 0.0 copy-done.3
  158.4 0.8 dynamic_slice.3
  159.1 0.0 copy-done.4
  159.1 0.1 broadcast_add_fusion
  159.2 16.7 %reduce-scatter.12.cloned.1.call-done = f32[16,2048]{1,0:T(8,128)} async-done(((f32[32,2048]{1,0:T(8,128)}), f32[16,2048]{1,0:T(8,128)}) %reduce-scatter.12.cloned.1.call-update) | async-done | bytes 131088
  175.9 1.2 copy.19
  177.1 0.3 fusion
  177.5 0.3 copy.12
  177.8 1.0 stack.3
  178.8 0.0 copy-start.1
  178.8 194.4 %all_to_all.16 = f32[64,16,2048]{2,1,0:T(8,128)S(1)} all-to-all(f32[64,16,2048]{2,1,0:T(8,128)S(1)} %stack.3), channel_id=1, replica_groups=mesh['gz_0'=8,'gz_1'=4,'gz_2'=2,'col'=4] {'gz_0','gz_1','gz_2'}, dimensions={0} | all-to-all | bytes 16777216 | tf_op jit(solution)/shard_map/all_to_all | solution.py:13
  373.2 0.0 copy-start.2
  373.2 0.0 copy-done.1
  373.2 5.6 %convolution_bitcast_fusion.1 = f32[64,2048]{1,0:T(8,128)S(1)} fusion(f32[1024,2048]{1,0:T(8,128)S(1)} %bitcast.38, f32[64,1024]{1,0:T(8,128)S(1)} %copy-done.1), kind=kOutput, calls=%fused_computation.1 | convolution fusion | flops 1610612736 | bytes 9175040 | tf_op jit(solution)/shard_map/dot_general | solution.py:82
  378.8 0.3 reshape.51
  379.1 0.0 copy-done.2
  379.1 1.0 fusion.4
  380.2 0.2 copy.27
  380.3 10.7 %all_to_all.17 = f32[4,64,512]{2,1,0:T(8,128)S(1)} all-to-all(f32[4,64,512]{2,1,0:T(8,128)S(1)} %bitcast.41), channel_id=1, replica_groups=mesh['gz_0'=8,'gz_1'=4,'gz_2'=2,'col'=4] {'col'}, dimensions={0} | all-to-all | bytes 1048576 | tf_op jit(solution)/shard_map/all_to_all | solution.py:47
  391.1 1.8 fusion.8
  (3 shorter events, 0.0 us)
Async XLA Ops:
  6.5 1.2 copy-start
  6.5 125.6 %reduce-scatter.8.cloned.1.call-start = ((), (), s32[]{:S(2)}) async-start(), calls=%async_computation.6 | async-start | bytes 9437184 | tf_op jit(solution)/shard_map/reduce_scatter | solution.py:35
  35.0 123.3 %copy-start.3 = (f32[512]{0:T(512)S(1)}, f32[512]{0:T(512)}, u32[]{:S(2)}) copy-start(f32[512]{0:T(512)} %param.13) | copy-start | bytes 6148
  35.0 124.1 %copy-start.4 = (f32[4]{0:T(128)S(1)}, f32[4]{0:T(128)}, u32[]{:S(2)}) copy-start(f32[4]{0:T(128)} %param.12) | copy-start | bytes 52
  35.0 123.3 %reduce-scatter.10.cloned.1.call-start = ((), (), s32[]{:S(2)}) async-start(), calls=%async_computation.7 | async-start | bytes 1310720
  134.7 41.2 %reduce-scatter.12.cloned.1.call-start = ((), (), s32[]{:S(2)}) async-start(), calls=%async_computation.8 | async-start | bytes 393216
  178.8 194.4 %copy-start.1 = (f32[64,1024]{1,0:T(8,128)S(1)}, f32[64,1024]{1,0:T(8,128)}, u32[]{:S(2)}) copy-start(f32[64,1024]{1,0:T(8,128)} %param.8) | copy-start | bytes 786436
  373.2 5.9 %copy-start.2 = (f32[4,4]{1,0:T(4,128)S(1)}, f32[4,4]{1,0:T(4,128)}, u32[]{:S(2)}) copy-start(f32[4,4]{1,0:T(4,128)} %param.9) | copy-start | bytes 196
Sparse Core Ops, SparseCore 0:
  35.2 96.9 reduce-scatter.7
  134.8 23.4 reduce-scatter.9
  160.8 15.0 reduce-scatter.11
